TPU v7x, 32 devices: a whole 2x2x4 slice. The times are simulated.
32 devices in a mesh: groups: 2 (over y), seq: 4 (over z), head: 4 (over x, core).
Axes of the slice: x: 2, y: 2, z: 4, core: 2. Of those that a mesh axis runs over, the one named last changes fastest.
Arguments:
- tile_tokens: bfloat16 [16, 256, 1536], P(('groups', 'seq')), parts along dimension 0, may hold values from -6 to 6
- tile_gain: float32 [1536], replicated, may hold values from 0.1 to 1.9
- w_gate_up: bfloat16 [2, 1536, 4096], P(None, 'seq', 'head'), may hold values from -0.15625 to 0.15625
- w_down: bfloat16 [4096, 1536], P('head', 'seq'), may hold values from -0.09375 to 0.09375
- layer_scale: float32 [1536], replicated, may hold values from 1 to 8
- fc_gain: float32 [1536], replicated, may hold values from 0.1 to 1.9
- w_embed: bfloat16 [1536, 768], P(None, 'head'), may hold values from -0.15625 to 0.15625
- embed_bias: float32 [768], P('head'), may hold values from -3 to 3
- pre_emb: bfloat16 [2032, 768], P(('groups', 'seq'), 'head'), parts along dimension 0, may hold values from -6 to 6
- tile_order: int32 [2048], P('groups'), parts along dimension 0, may hold values from 0 to 1023, as said below
- valid_count: int32 [2], P('groups'), parts along dimension 0, may hold values from 256 to 1024
- slide_gain: float32 [768], replicated, may hold values from 0.1 to 1.9
- w_qkv: bfloat16 [3, 768, 768], P(None, None, 'head'), may hold values from -1.25 to 1.25
- sub_gain: float32 [768], P('head'), may hold values from 0.1 to 1.9
- w_out: bfloat16 [768, 768], P('head'), may hold values from -0.21875 to 0.21875
Outputs:
- mixed: float32 [2048, 768], P(('groups', 'seq'), 'head'), parts along dimension 0
There are 2 independent parts, one for each index of `groups`. A program takes and returns all parts, laid end to end along the dimension named above; an argument that names none is the same for every part. Nothing has to cross between parts.
Inputs may be any that keep to these rules, and one draw needn't show every extreme that they name: `tile_order`: A permutation of 0 to 1023. For every block of 256 positions (d * 256 to (d + 1) * 256 - 1) and every block of 256 stored rows, exactly 64 positions of the first take rows of the second.
All inputs are finite; a program needn't handle non-finite values.
Results may differ from a plain program's by a relative error of at most 0.0046.
Values may be sent and summed in bfloat16 or wider, within the bound.
No kernel may reach another device: no remote copies, remote signals or barrier semaphores. Data moves between devices by JAX's collectives and lax.ppermute only.
A program may use at most 64 MiB of HBM per device.

v0:
```python
import math

import jax
import jax.numpy as jnp
from jax import lax
from jax.sharding import PartitionSpec as P

DS = 768
HEAD_DIM = 48
SPAN0 = 1024
SPAN1 = 4096
DILATION_SECOND = 4
DILATION_THIRD = 16


layer_eps = 1e-05
masked_score = -1e30


def from_partner(value, axis, bit):
    mask = 2**bit
    pairs = [(source, source ^ mask) for source in range(lax.axis_size(axis))]
    return lax.ppermute(value, axis, pairs)


def normalize(values, gain):
    centered = values - jnp.mean(values, axis=-1, keepdims=True)
    variance = jnp.mean(centered * centered, axis=-1, keepdims=True)
    return centered * lax.rsqrt(variance + layer_eps) * gain


def select_rows(stacked, dilation, offsets):
    group_count, row_count, row_width = stacked.shape
    head_count = offsets.shape[0]
    arranged = stacked.reshape(
        group_count, row_count // dilation, dilation, head_count, row_width // head_count
    )
    choose = jnp.arange(dilation, dtype=jnp.int32)[:, None] == offsets[None, :]
    chosen = jnp.sum(
        jnp.where(choose[None, None, :, :, None], arranged, jnp.zeros((), stacked.dtype)), axis=2
    )
    return chosen.reshape(group_count, row_count // dilation, row_width)


def scatter_rows(attended, log_mass, dilation, offsets):
    query_count, head_count, head_size = attended.shape
    choose = jnp.arange(dilation, dtype=jnp.int32)[:, None] == offsets[None, :]
    spread_out = jnp.where(choose[None, :, :, None], attended[:, None, :, :], 0.0).reshape(
        query_count * dilation, head_count, head_size
    )
    spread_mass = jnp.where(choose[None, :, :], log_mass[:, None, :], masked_score).reshape(
        query_count * dilation, head_count
    )
    selected = jnp.broadcast_to(choose[None, :, :], (query_count, dilation, head_count)).reshape(
        query_count * dilation, head_count
    )
    return (spread_out, spread_mass, selected)


def attend(query_rows, key_rows, value_rows, positions, valid_limit, head_count):
    head_size = query_rows.shape[1] // head_count
    query_heads = query_rows.reshape(query_rows.shape[0], head_count, head_size)
    key_heads = key_rows.reshape(key_rows.shape[0], head_count, head_size)
    value_heads = value_rows.reshape(value_rows.shape[0], head_count, head_size)
    scores = jnp.einsum(
        "qhe,khe->hqk", query_heads, key_heads, preferred_element_type=jnp.float32
    ) / math.sqrt(head_size)
    scores = jnp.where((positions < valid_limit)[:, None, :], scores, masked_score)
    highest = jnp.max(scores, axis=-1, keepdims=True)
    exponent = jnp.exp(scores - highest)
    mass_sum = jnp.sum(exponent, axis=-1, keepdims=True)
    weights = (exponent / mass_sum).astype(jnp.bfloat16)
    attended = jnp.einsum("hqk,khe->qhe", weights, value_heads, preferred_element_type=jnp.float32)
    return (attended, (highest[..., 0] + jnp.log(mass_sum[..., 0])).T)


def body(
    tile_tokens,
    tile_gain,
    w_gate_up,
    w_down,
    layer_scale,
    fc_gain,
    w_embed,
    embed_bias,
    pre_emb,
    tile_order,
    valid_count,
    slide_gain,
    w_qkv,
    sub_gain,
    w_out,
):
    new_count, patch_count, tile_width = tile_tokens.shape
    token_rows = tile_tokens.reshape(new_count * patch_count, tile_width)
    normed = normalize(token_rows.astype(jnp.float32), tile_gain).astype(jnp.bfloat16)
    hidden_width = w_gate_up.shape[2]
    gate_up = jnp.einsum(
        "rk,gkf->grf",
        normed,
        lax.all_gather(w_gate_up, "seq", axis=1, tiled=True),
        preferred_element_type=jnp.float32,
    )
    hidden = (jax.nn.silu(gate_up[0]) * gate_up[1]).astype(jnp.bfloat16)
    pooled_hidden = jnp.mean(
        hidden.reshape(new_count, patch_count, hidden_width), axis=1, dtype=jnp.float32
    )
    everyone = lax.all_gather(pooled_hidden, "seq", axis=0, tiled=True)
    local_part = jnp.dot(everyone, w_down.astype(jnp.float32), precision=lax.Precision.HIGHEST)
    pooled_part = lax.all_to_all(local_part, "seq", split_axis=0, concat_axis=1, tiled=True)
    summed = lax.psum(pooled_part, "head")
    pooled = jnp.mean(tile_tokens, axis=1, dtype=jnp.float32) + layer_scale * summed
    feature = normalize(pooled, fc_gain).astype(jnp.bfloat16)
    new_rows = (jnp.dot(feature, w_embed, preferred_element_type=jnp.float32) + embed_bias).astype(
        jnp.bfloat16
    )
    stored = jnp.concatenate([new_rows, pre_emb], axis=0)
    block_rows = stored.shape[0]
    total_rows = tile_order.shape[0]
    peer_rows = block_rows // lax.axis_size("seq")
    device = lax.axis_index("seq")
    local_index = jnp.arange(block_rows, dtype=jnp.int32)
    inverse = (
        jnp.zeros((total_rows,), jnp.int32)
        .at[tile_order]
        .set(jnp.arange(total_rows, dtype=jnp.int32))
    )
    placed = lax.dynamic_slice_in_dim(inverse, device * block_rows, block_rows)
    target = placed // block_rows
    before = (target[:, None] == target[None, :]) & (placed[None, :] < placed[:, None])
    slot_index = target * peer_rows + jnp.sum(before, axis=1, dtype=jnp.int32)
    routing = (slot_index[None, :] == local_index[:, None]).astype(jnp.bfloat16)
    outgoing = jnp.dot(routing, stored, preferred_element_type=jnp.float32).astype(jnp.bfloat16)
    incoming = lax.all_to_all(outgoing, "seq", split_axis=0, concat_axis=0, tiled=True)
    wanted = lax.dynamic_slice_in_dim(tile_order, device * block_rows, block_rows)
    source = wanted // block_rows
    earlier = (source[:, None] == source[None, :]) & (local_index[None, :] < local_index[:, None])
    arrival = source * peer_rows + jnp.sum(earlier, axis=1, dtype=jnp.int32)
    own_part = jnp.take(incoming, arrival, axis=0)
    sequence = lax.all_gather(own_part, "head", axis=1, tiled=True)
    slide_normed = normalize(sequence.astype(jnp.float32), slide_gain).astype(jnp.bfloat16)
    projected_rows = jnp.einsum(
        "rd,gdc->grc", slide_normed, w_qkv, preferred_element_type=jnp.float32
    ).astype(jnp.bfloat16)
    cols_here = projected_rows.shape[2]
    head_count = cols_here // HEAD_DIM
    head_indices = lax.axis_index("head") * head_count + jnp.arange(head_count, dtype=jnp.int32)
    valid_limit = valid_count[0]
    row_index = device * block_rows + local_index
    near_devices = min(SPAN0, total_rows) // block_rows
    near_rows = projected_rows[1:]
    for bit_index in range(near_devices.bit_length() - 1):
        partner = from_partner(near_rows, "seq", bit_index)
        upper_half = device // (1 << bit_index) % 2 == 1
        near_rows = jnp.where(
            upper_half,
            jnp.concatenate([partner, near_rows], 1),
            jnp.concatenate([near_rows, partner], 1),
        )
    near_start = device // near_devices * near_devices * block_rows
    near_pos = jnp.broadcast_to(
        near_start + jnp.arange(near_rows.shape[1], dtype=jnp.int32),
        (head_count, near_rows.shape[1]),
    )
    near_out, near_mass = attend(
        projected_rows[0], near_rows[0], near_rows[1], near_pos, valid_limit, head_count
    )
    near_sel = jnp.ones((block_rows, head_count), dtype=bool)
    middle_level_offsets = head_indices % DILATION_SECOND
    middle_level = select_rows(projected_rows, DILATION_SECOND, middle_level_offsets)
    middle_devices = min(SPAN1, total_rows) // block_rows
    middle_key_value = middle_level[1:]
    every_row = lax.all_gather(middle_key_value, "seq", axis=1, tiled=True)
    group_rows = middle_devices * middle_key_value.shape[1]
    middle_key_value = lax.dynamic_slice_in_dim(
        every_row, device // middle_devices * group_rows, group_rows, 1
    )
    middle_start = device // middle_devices * middle_devices * block_rows
    middle_pos = (
        middle_start
        + middle_level_offsets[:, None]
        + DILATION_SECOND * jnp.arange(middle_key_value.shape[1], dtype=jnp.int32)[None, :]
    )
    middle_attention, middle_log_sum = attend(
        middle_level[0],
        middle_key_value[0],
        middle_key_value[1],
        middle_pos,
        valid_limit,
        head_count,
    )
    middle_output, middle_level_mass, middle_selected = scatter_rows(
        middle_attention, middle_log_sum, DILATION_SECOND, middle_level_offsets
    )
    distant_offsets = head_indices % DILATION_THIRD
    distant_local_rows = select_rows(projected_rows, DILATION_THIRD, distant_offsets)
    distant_key_value = lax.all_gather(distant_local_rows[1:], "seq", axis=1, tiled=True)
    distant_positions = (
        distant_offsets[:, None]
        + DILATION_THIRD * jnp.arange(distant_key_value.shape[1], dtype=jnp.int32)[None, :]
    )
    distant_attention, distant_log_sum = attend(
        distant_local_rows[0],
        distant_key_value[0],
        distant_key_value[1],
        distant_positions,
        valid_limit,
        head_count,
    )
    distant_output, distant_mass, distant_selected = scatter_rows(
        distant_attention, distant_log_sum, DILATION_THIRD, distant_offsets
    )
    outputs = jnp.stack([near_out, middle_output, distant_output])
    masses = jnp.stack([near_mass, middle_level_mass, distant_mass])
    selects = jnp.stack([near_sel, middle_selected, distant_selected])
    ceiling = jnp.max(masses, axis=0)
    shares = jnp.where(selects, jnp.exp(masses - ceiling), 0.0)
    combined = jnp.sum(shares[..., None] * outputs, axis=0) / jnp.sum(shares, axis=0)[..., None]
    combined = jnp.where((row_index < valid_limit)[:, None, None], combined, 0.0).reshape(
        block_rows, cols_here
    )
    row_total, row_square = lax.psum(
        (jnp.sum(combined, axis=1), jnp.sum(combined * combined, axis=1)), "head"
    )
    mean_value = row_total / DS
    mean_square = row_square / DS
    scaling = lax.rsqrt(mean_square - mean_value * mean_value + layer_eps)
    settled = ((combined - mean_value[:, None]) * scaling[:, None] * sub_gain).astype(jnp.bfloat16)
    partial_rows = jnp.dot(settled, w_out, preferred_element_type=jnp.float32)
    branch_sum = lax.psum_scatter(partial_rows, "head", scatter_dimension=1, tiled=True)
    return own_part.astype(jnp.float32) + branch_sum


def solution(mesh):
    placed = (
        P(("groups", "seq"), None, None),
        P(),
        P(None, "seq", "head"),
        P("head", "seq"),
        P(),
        P(),
        P(None, "head"),
        P("head"),
        P(("groups", "seq"), "head"),
        P("groups"),
        P("groups"),
        P(),
        P(None, None, "head"),
        P("head"),
        P("head", None),
    )
    return jax.shard_map(
        body, mesh=mesh, in_specs=placed, out_specs=P(("groups", "seq"), "head"), check_vma=False
    )
```

profile of v0, /device:TPU:0, one launch (start us, length us, event | category | flops | bytes accessed | tf_op | source)
XLA Modules:
  0.0 281.4 jit_solution(12463239555199441893)
XLA Ops:
  6.6 0.7 all-gather.3.cloned.1.call-update
  7.3 2.0 convert_reduce_fusion.1
  9.3 0.5 multiply_reduce_fusion
  10.5 4.3 %scatter_custom_fusion = s32[1024]{0:T(1024)S(1)} fusion(s32[1024]{0:T(1024)S(1)} %compare_select_fusion, s32[1024]{0:T(1024)S(1)} %iota.73, s32[]{:T(128)} %constant.151.clone.1), kind=kCustom, calls=%fused_computation.103 | custom fusion | bytes 4100 | tf_op jit(solution)/shard_map/scatter | solution.py:126
  15.0 0.2 convert_reduce_fusion.5
  15.2 0.2 convert_reduce_fusion.4
  15.6 1.7 fusion.4
  17.3 109.7 %all-gather.3.cloned.1.call-done = bf16[2,1536,1024]{2,1,0:T(8,128)(2,1)} async-done(((bf16[2,384,1024]{2,1,0:T(8,128)(2,1)}), bf16[2,1536,1024]{2,1,0:T(8,128)(2,1)}) %all-gather.3.cloned.1.call-update) | async-done | bytes 6291472 | tf_op jit(solution)/shard_map/all_gather | solution.py:101
  127.0 6.0 %convolution_bitcast_fusion = f32[2,512,1024]{2,1,0:T(8,128)S(1)} fusion(bf16[2,1536,1024]{2,1,0:T(8,128)(2,1)} %all-gather.3.cloned.1.call-done, bf16[512,1536]{1,0:T(8,128)(2,1)} %fusion.4), kind=kOutput, calls=%fused_computation.14 | convolution fusion | flops 3221225472 | bytes 12058624 | tf_op jit(solution)/shard_map/rk,gkf->grf/dot_general | solution.py:98
  133.0 0.6 fusion.51
  133.6 0.6 convert_reduce_fusion.2
  134.2 13.2 %all-gather = f32[4,2,1024]{2,1,0:T(2,128)S(1)} all-gather(f32[1,2,1024]{2,1,0:T(2,128)S(1)} %multiply_bitcast_fusion), channel_id=1, replica_groups=mesh['groups'=2,'seq'=4,'head'=4] {'seq'}, dimensions={0}, use_global_device_ids=true | all-gather | bytes 40960 | tf_op jit(solution)/shard_map/all_gather | solution.py:108
  147.5 0.4 fusion.57
  147.9 0.6 all_to_all.22
  148.5 3.3 %all-to-all-start = ((f32[4,2,384]{2,1,0:T(2,128)}), f32[4,2,384]{2,1,0:T(2,128)S(1)}, u32[]{:S(2)}, u32[]{:S(2)}) async-start(f32[4,2,384]{2,1,0:T(2,128)} %all_to_all.22), calls=%async_computation | async-start | bytes 24576 | tf_op jit(solution)/shard_map/all_to_all | solution.py:110
  151.8 5.6 %all-to-all-done = f32[4,2,384]{2,1,0:T(2,128)S(1)} async-done(((f32[4,2,384]{2,1,0:T(2,128)}), f32[4,2,384]{2,1,0:T(2,128)S(1)}, u32[]{:S(2)}, u32[]{:S(2)}) %all-to-all-start) | async-done | bytes 12320 | tf_op jit(solution)/shard_map/all_to_all | solution.py:110
  157.3 10.1 %psum.21 = f32[2,1536]{1,0:T(2,128)S(1)} all-reduce(f32[2,1536]{1,0:T(2,128)S(1)} %bitcast.134), channel_id=1, replica_groups=mesh['groups'=2,'seq'=4,'head'=4] {'head'}, use_global_device_ids=true, to_apply=%region_7.8 | all-reduce | flops 3072 | bytes 24576 | tf_op jit(solution)/shard_map/psum | solution.py:111
  167.6 0.2 multiply_reduce_fusion.2
  167.8 0.3 fusion.10
  168.3 0.2 convolution_convert_fusion
  168.5 0.8 copy.71
  169.3 3.3 %all-to-all-start.1 = ((bf16[4,64,192]{2,1,0:T(8,128)(2,1)}), bf16[4,64,192]{2,1,0:T(8,128)(2,1)S(1)}, u32[]{:S(2)}, u32[]{:S(2)}) async-start(bf16[4,64,192]{2,1,0:T(8,128)(2,1)} %bitcast.8), calls=%async_computation.1 | async-start | bytes 262144 | tf_op jit(solution)/shard_map/all_to_all | solution.py:134
  173.4 5.2 %all-to-all-done.1 = bf16[4,64,192]{2,1,0:T(8,128)(2,1)S(1)} async-done(((bf16[4,64,192]{2,1,0:T(8,128)(2,1)}), bf16[4,64,192]{2,1,0:T(8,128)(2,1)S(1)}, u32[]{:S(2)}, u32[]{:S(2)}) %all-to-all-start.1) | async-done | bytes 98336 | tf_op jit(solution)/shard_map/all_to_all | solution.py:134
  178.6 1.2 gather_fusion
  179.9 6.4 %all_gather.17 = bf16[256,768]{0,1:T(8,128)(2,1)S(1)} all-gather(bf16[256,192]{0,1:T(8,128)(2,1)S(1)} %broadcast_select_fusion.2), channel_id=1, replica_groups=mesh['groups'=2,'seq'=4,'head'=4] {'head'}, dimensions={1}, use_global_device_ids=true | all-gather | bytes 491520 | tf_op jit(solution)/shard_map/all_gather | solution.py:140
  186.6 0.5 fusion.17
  187.4 0.4 reshape.504
  187.8 0.7 select_reduce_fusion.1
  188.8 14.0 %all_gather.18 = bf16[2,256,192]{2,0,1:T(2,128)(2,1)S(1)} all-gather(bf16[2,64,192]{2,0,1:T(2,128)(2,1)S(1)} %copy.79), channel_id=1, replica_groups=mesh['groups'=2,'seq'=4,'head'=4] {'seq'}, dimensions={1}, use_global_device_ids=true | all-gather | bytes 245760 | tf_op jit(solution)/shard_map/all_gather | solution.py:173
  202.9 0.4 fusion.53
  203.5 0.3 fusion.56
  204.4 0.4 reshape.505
  204.8 0.6 select_reduce_fusion
  205.5 13.3 %all_gather.19 = bf16[2,64,192]{2,1,0:T(8,128)(2,1)S(1)} all-gather(bf16[2,16,192]{2,1,0:T(8,128)(2,1)S(1)} %slice.61), channel_id=1, replica_groups=mesh['groups'=2,'seq'=4,'head'=4] {'seq'}, dimensions={1}, use_global_device_ids=true | all-gather | bytes 61440 | tf_op jit(solution)/shard_map/all_gather | solution.py:197
  218.9 0.2 fusion.55
  219.8 0.3 convolution_bitcast_fusion.1
  220.6 0.2 convolution_bitcast_fusion.2
  221.1 6.2 %collective-permute-done = bf16[2,256,192]{1,2,0:T(8,128)(2,1)S(1)} collective-permute-done((bf16[2,256,192]{1,2,0:T(8,128)(2,1)S(1)}, bf16[2,256,192]{1,2,0:T(8,128)(2,1)S(1)}, u32[]{:S(2)}, u32[]{:S(2)}) %collective-permute-start) | collective-permute-done | bytes 196640 | tf_op jit(solution)/shard_map/ppermute | solution.py:23
  227.3 0.8 collective-permute-start.1
  228.2 11.7 %collective-permute-done.1 = bf16[2,512,192]{1,2,0:T(8,128)(2,1)S(1)} collective-permute-done((bf16[2,512,192]{1,2,0:T(8,128)(2,1)S(1)}, bf16[2,512,192]{1,2,0:T(8,128)(2,1)S(1)}, u32[]{:S(2)}, u32[]{:S(2)}) %collective-permute-start.1) | collective-permute-done | bytes 393248 | tf_op jit(solution)/shard_map/ppermute | solution.py:23
  239.9 0.2 maximum_select_fusion
  240.2 0.9 fusion
  241.0 1.0 fusion.1
  242.1 1.2 fusion.8
  243.6 5.7 %all-reduce = (f32[256]{0:T(256)S(1)}, f32[256]{0:T(256)S(1)}) all-reduce(f32[256]{0:T(256)S(1)} %get-tuple-element.8, f32[256]{0:T(256)S(1)} %get-tuple-element.7), channel_id=1, replica_groups=mesh['groups'=2,'seq'=4,'head'=4] {'head'}, use_global_device_ids=true, to_apply=%region_25.26 | all-reduce | flops 512 | bytes 4096 | tf_op jit(solution)/shard_map/psum | solution.py:222
  249.4 1.2 fusion.58
  250.6 22.4 %reduce-scatter.2.cloned.1.call-done = f32[256,192]{0,1:T(8,128)} async-done(((f32[256,768]{0,1:T(8,128)}), f32[256,192]{0,1:T(8,128)}) %reduce-scatter.2.cloned.1.call-update) | async-done | bytes 196624 | tf_op jit(solution)/shard_map/reduce_scatter | solution.py:230
  273.0 1.6 convert_add_fusion
  (119 shorter events, 5.3 us)
Async XLA Ops:
  6.5 180.1 %copy-start = (bf16[3,768,192]{1,2,0:T(8,128)(2,1)S(1)}, bf16[3,768,192]{1,2,0:T(8,128)(2,1)}, u32[]{:S(2)}) copy-start(bf16[3,768,192]{1,2,0:T(8,128)(2,1)} %param.27) | copy-start | bytes 2654212
  6.5 2.7 copy-start.1
  6.5 4.0 %copy-start.7 = (s32[1024]{0:T(1024)S(1)}, s32[1024]{0:T(1024)}, u32[]{:S(2)}) copy-start(s32[1024]{0:T(1024)} %param.24) | copy-start | bytes 12292
  6.5 9.1 %copy-start.5 = (f32[1536]{0:T(1024)S(1)}, f32[1536]{0:T(1024)}, u32[]{:S(2)}) copy-start(f32[1536]{0:T(1024)} %param.16) | copy-start | bytes 18436
  6.5 120.5 %all-gather.3.cloned.1.call-start = ((), (), s32[]{:S(2)}) async-start(), calls=%async_computation.3 | async-start | bytes 7864320 | tf_op jit(solution)/shard_map/all_gather | solution.py:101
  133.6 13.9 %copy-start.3 = (bf16[1024,384]{1,0:T(8,128)(2,1)S(1)}, bf16[1024,384]{1,0:T(8,128)(2,1)}, u32[]{:S(2)}) copy-start(bf16[1024,384]{1,0:T(8,128)(2,1)} %param.18) | copy-start | bytes 2359300
  133.6 33.9 %copy-start.6 = (f32[1536]{0:T(1024)S(1)}, f32[1536]{0:T(1024)}, u32[]{:S(2)}) copy-start(f32[1536]{0:T(1024)} %param.19) | copy-start | bytes 18436
  133.6 34.2 %copy-start.9 = (bf16[1536,192]{0,1:T(8,128)(2,1)S(1)}, bf16[1536,192]{0,1:T(8,128)(2,1)}, u32[]{:S(2)}) copy-start(bf16[1536,192]{0,1:T(8,128)(2,1)} %param.21) | copy-start | bytes 1769476
  133.6 34.2 %copy-start.11 = (f32[1536]{0:T(1024)S(1)}, f32[1536]{0:T(1024)}, u32[]{:S(2)}) copy-start(f32[1536]{0:T(1024)} %param.20) | copy-start | bytes 18436
  133.6 34.2 %copy-start.13 = (f32[192]{0:T(256)S(1)}, f32[192]{0:T(256)}, u32[]{:S(2)}) copy-start(f32[192]{0:T(256)} %param.22) | copy-start | bytes 2308
  133.6 34.7 %copy-start.10 = (bf16[254,192]{0,1:T(8,128)(2,1)S(1)}, bf16[254,192]{0,1:T(8,128)(2,1)}, u32[]{:S(2)}) copy-start(bf16[254,192]{0,1:T(8,128)(2,1)} %param.23) | copy-start | bytes 292612
  134.2 52.4 %copy-start.12 = (f32[768]{0:T(1024)S(1)}, f32[768]{0:T(1024)}, u32[]{:S(2)}) copy-start(f32[768]{0:T(1024)} %param.26) | copy-start | bytes 9220
  148.5 8.8 %all-to-all-start = ((f32[4,2,384]{2,1,0:T(2,128)}), f32[4,2,384]{2,1,0:T(2,128)S(1)}, u32[]{:S(2)}, u32[]{:S(2)}) async-start(f32[4,2,384]{2,1,0:T(2,128)} %all_to_all.22), calls=%async_computation | async-start | bytes 24576 | tf_op jit(solution)/shard_map/all_to_all | solution.py:110
  169.3 9.4 %all-to-all-start.1 = ((bf16[4,64,192]{2,1,0:T(8,128)(2,1)}), bf16[4,64,192]{2,1,0:T(8,128)(2,1)S(1)}, u32[]{:S(2)}, u32[]{:S(2)}) async-start(bf16[4,64,192]{2,1,0:T(8,128)(2,1)} %bitcast.8), calls=%async_computation.1 | async-start | bytes 262144 | tf_op jit(solution)/shard_map/all_to_all | solution.py:134
  172.6 100.4 %reduce-scatter.2.cloned.1.call-start = ((), (), s32[]{:S(2)}) async-start(), calls=%async_computation.4 | async-start | bytes 983040 | tf_op jit(solution)/shard_map/reduce_scatter | solution.py:230
  187.2 16.6 %copy-start.2 = (bf16[3,256,192]{1,2,0:T(8,128)(2,1)}, bf16[3,256,192]{1,2,0:T(8,128)(2,1)S(1)}, u32[]{:S(2)}) copy-start(bf16[3,256,192]{1,2,0:T(8,128)(2,1)S(1)} %convert_bitcast_fusion) | copy-start | bytes 884740
  219.6 7.7 %collective-permute-start = (bf16[2,256,192]{1,2,0:T(8,128)(2,1)S(1)}, bf16[2,256,192]{1,2,0:T(8,128)(2,1)S(1)}, u32[]{:S(2)}, u32[]{:S(2)}) collective-permute-start(bf16[2,256,192]{1,2,0:T(8,128)(2,1)S(1)} %slice.71), channel_id=1, source_target_pairs={{0,4},{4,0},{8,12},{12,8},{1,5},{5,1},{9,13},{13,9},{2,6},{6,2},{1... | collective-permute-start | bytes 589832 | tf_op jit(solution)/shard_map/ppermute | solution.py:23
  220.5 19.7 %slice-start = ((bf16[3,256,192]{1,2,0:T(8,128)(2,1)}), bf16[1,256,192]{1,2,0:T(8,128)(2,1)S(1)}, s32[]{:S(2)}) async-start(bf16[3,256,192]{1,2,0:T(8,128)(2,1)} %copy-done.2), calls=%async_computation.5 | async-start | bytes 196608 | tf_op jit(solution)/shard_map/slice | solution.py:166
  227.3 12.5 %collective-permute-start.1 = (bf16[2,512,192]{1,2,0:T(8,128)(2,1)S(1)}, bf16[2,512,192]{1,2,0:T(8,128)(2,1)S(1)}, u32[]{:S(2)}, u32[]{:S(2)}) collective-permute-start(bf16[2,512,192]{1,2,0:T(8,128)(2,1)S(1)} %maximum_select_fusion.1), channel_id=1, source_target_pairs={{0,8},{4,12},{8,0},{12,4},{1,9},{5,13},{9,1},{13,5},{2,10},{6,14},... | collective-permute-start | bytes 1179656 | tf_op jit(solution)/shard_map/ppermute | solution.py:23
  242.1 7.2 %copy-start.8 = (f32[192]{0:T(256)S(1)}, f32[192]{0:T(256)}, u32[]{:S(2)}) copy-start(f32[192]{0:T(256)} %param.28) | copy-start | bytes 2308
  242.1 7.3 %copy-start.4 = (bf16[192,768]{1,0:T(8,128)(2,1)S(1)}, bf16[192,768]{1,0:T(8,128)(2,1)}, u32[]{:S(2)}) copy-start(bf16[192,768]{1,0:T(8,128)(2,1)} %param.29) | copy-start | bytes 884740
Sparse Core Ops, SparseCore 0:
  8.9 118.0 all-gather.2
  250.7 22.2 reduce-scatter.1
where the time goes:
time: 282 us; the launch traced here: 281 us
  waiting for transfers between devices  161 us (57%)
  blocking collectives  62.7 us (22%)
  between operations  14.7 us (5%)
  local copies, waits for them, and re-layouts  12.1 us (4%)
  matrix products  11.7 us (4%)
  other arithmetic  11.2 us (4%)
  starting transfers between devices  7.51 us (3%)
    all_gather x1, waiting for transfers between devices, body(): lax.all_gather(w_gate_up, 'seq', axis=1, tiled=True)  110 us
    reduce_scatter x1, waiting for transfers between devices, body(): lax.psum_scatter(partial_rows, 'head', scatter_dimension=1, tiled=True)  22.4 us
    ppermute x2, waiting for transfers between devices, from_partner(): return lax.ppermute(value, axis, pairs)  17.9 us
    all_gather x1, blocking collectives, body(): every_row = lax.all_gather(middle_key_value, 'seq', axis=1, tiled=True)  14 us
    all_gather x1, blocking collectives, body(): lax.all_gather(distant_local_rows[1:], 'seq', axis=1, tiled=True)  13.3 us
    all_gather x1, blocking collectives, body(): everyone = lax.all_gather(pooled_hidden, 'seq', axis=0, tiled=True)  13.2 us
    psum x1, blocking collectives, body(): summed = lax.psum(pooled_part, 'head')  10.1 us
    all_gather x1, blocking collectives, body(): sequence = lax.all_gather(own_part, 'head', axis=1, tiled=True)  6.37 us
  transfers between devices with their start and end apart: 6, of which 6 were waited for; matrix products, arithmetic and copies ran while one was open for 4% of the time, Pallas kernels for 0%

commit v1 on v0

--- a/solution.py
+++ b/solution.py
@@ -231,6 +231,161 @@
     return own_part.astype(jnp.float32) + branch_sum
 
 
+def spread(value, axis):
+    count = lax.axis_size(axis)
+    return lax.all_to_all(
+        jnp.broadcast_to(value[None], (count, *value.shape)), axis, split_axis=0, concat_axis=0
+    )
+
+
+def hidden_means(tile_tokens, tile_gain, w_gate_up, early):
+    new_count, patch_count, tile_width = tile_tokens.shape
+    token_rows = tile_tokens.reshape(new_count * patch_count, tile_width)
+    normed = normalize(token_rows.astype(jnp.float32), tile_gain).astype(jnp.bfloat16)
+    gathered = lax.all_gather(w_gate_up, "seq", axis=1, tiled=True)
+    gathered, early = lax.optimization_barrier((gathered, early))
+    gate_up = jnp.einsum("rk,gkf->grf", normed, gathered, preferred_element_type=jnp.float32)
+    hidden = (jax.nn.silu(gate_up[0]) * gate_up[1]).astype(jnp.bfloat16)
+    pooled_hidden = jnp.mean(
+        hidden.reshape(new_count, patch_count, hidden.shape[1]), axis=1, dtype=jnp.float32
+    )
+    everyone = spread(pooled_hidden, "seq")
+    return everyone.reshape(-1, hidden.shape[1]), early
+
+
+def body_single(
+    tile_tokens,
+    tile_gain,
+    w_gate_up,
+    w_down,
+    layer_scale,
+    fc_gain,
+    w_embed,
+    embed_bias,
+    pre_emb,
+    tile_order,
+    valid_count,
+    slide_gain,
+    w_qkv,
+    sub_gain,
+    w_out,
+):
+    new_count = tile_tokens.shape[0]
+    seq_size = lax.axis_size("seq")
+    head_size = lax.axis_size("head")
+    device = lax.axis_index("seq")
+    valid_limit = valid_count[0]
+    stored = jnp.concatenate([jnp.zeros((new_count, pre_emb.shape[1]), pre_emb.dtype), pre_emb], 0)
+    block_rows = stored.shape[0]
+    total_rows = tile_order.shape[0]
+    peer_rows = block_rows // seq_size
+    local_index = jnp.arange(block_rows, dtype=jnp.int32)
+    own_rows = device * block_rows + local_index
+    hits = tile_order[None, :] == own_rows[:, None]
+    placed = jnp.sum(
+        jnp.where(hits, jnp.arange(total_rows, dtype=jnp.int32)[None, :], 0), axis=1, dtype=jnp.int32
+    )
+    target = placed // block_rows
+    before = (target[:, None] == target[None, :]) & (placed[None, :] < placed[:, None])
+    slot_index = target * peer_rows + jnp.sum(before, axis=1, dtype=jnp.int32)
+    routing = (slot_index[None, :] == local_index[:, None]).astype(jnp.bfloat16)
+    outgoing = jnp.dot(routing, stored, preferred_element_type=jnp.float32).astype(jnp.bfloat16)
+    incoming = lax.all_to_all(outgoing, "seq", split_axis=0, concat_axis=0, tiled=True)
+    wanted = lax.dynamic_slice_in_dim(tile_order, device * block_rows, block_rows)
+    source = wanted // block_rows
+    earlier = (source[:, None] == source[None, :]) & (local_index[None, :] < local_index[:, None])
+    arrival = source * peer_rows + jnp.sum(earlier, axis=1, dtype=jnp.int32)
+    arranging = (arrival[:, None] == local_index[None, :]).astype(jnp.bfloat16)
+    own_pre = jnp.dot(arranging, incoming, preferred_element_type=jnp.float32).astype(jnp.bfloat16)
+    sequence = lax.all_gather(own_pre, "head", axis=1, tiled=True)
+
+    def project(rows):
+        rows_normed = normalize(rows.astype(jnp.float32), slide_gain).astype(jnp.bfloat16)
+        return jnp.einsum(
+            "rd,gdc->grc", rows_normed, w_qkv, preferred_element_type=jnp.float32
+        ).astype(jnp.bfloat16)
+
+    projected_pre = project(sequence)
+    key_value_pre = lax.all_gather(projected_pre[1:], "seq", axis=1, tiled=True)
+    out_columns = lax.all_to_all(w_out, "head", split_axis=1, concat_axis=0, tiled=True)
+    all_gain = lax.all_gather(sub_gain, "head", axis=0, tiled=True)
+    token_means = lax.all_gather(
+        jnp.mean(tile_tokens, axis=1, dtype=jnp.float32), "seq", axis=0, tiled=True
+    )
+    tile_count = token_means.shape[0]
+    in_block = tile_order % block_rows
+    tile_of = jnp.where(
+        in_block < new_count, tile_order // block_rows * new_count + in_block, tile_count
+    )
+    holds = (tile_of[:, None] == jnp.arange(tile_count, dtype=jnp.int32)[None, :]).astype(
+        jnp.bfloat16
+    )
+    holds_own = lax.dynamic_slice_in_dim(holds, device * block_rows, block_rows)
+
+    early = (own_pre, projected_pre, key_value_pre, out_columns, all_gain, token_means)
+    everyone, early = hidden_means(tile_tokens, tile_gain, w_gate_up, early)
+    own_pre, projected_pre, key_value_pre, out_columns, all_gain, token_means = early
+    local_part = jnp.dot(everyone, w_down.astype(jnp.float32), precision=lax.Precision.HIGHEST)
+    parts = lax.all_gather(local_part, ("seq", "head"))
+    summed = jnp.sum(parts.reshape(seq_size, head_size, tile_count, -1), axis=1)
+    summed = summed.transpose(1, 0, 2).reshape(tile_count, -1)
+    pooled = token_means + layer_scale * summed
+    feature = normalize(pooled, fc_gain).astype(jnp.bfloat16)
+    new_rows = (jnp.dot(feature, w_embed, preferred_element_type=jnp.float32) + embed_bias).astype(
+        jnp.bfloat16
+    )
+    new_full = lax.all_gather(new_rows, "head", axis=1, tiled=True)
+    projected_new = project(new_full)
+
+    def place(held, rows):
+        return jnp.dot(held, rows, preferred_element_type=jnp.float32).astype(jnp.bfloat16)
+
+    own_part = own_pre + place(holds_own, new_rows)
+    query = projected_pre[0] + place(holds_own, projected_new[0])
+    key = key_value_pre[0] + place(holds, projected_new[1])
+    value = key_value_pre[1] + place(holds, projected_new[2])
+    cols_here = query.shape[1]
+    head_count = cols_here // HEAD_DIM
+    row_index = own_rows
+    key_index = jnp.arange(total_rows, dtype=jnp.int32)
+    key_valid = key_index < valid_limit
+    attended = []
+    for head in range(head_count):
+        columns = slice(head * HEAD_DIM, (head + 1) * HEAD_DIM)
+        head_index = lax.axis_index("head") * head_count + head
+        scores = lax.dot_general(
+            query[:, columns],
+            key[:, columns],
+            (((1,), (1,)), ((), ())),
+            preferred_element_type=jnp.float32,
+        ) / math.sqrt(HEAD_DIM)
+        scores = jnp.where(key_valid[None, :], scores, masked_score)
+        highest = jnp.max(scores, axis=1, keepdims=True)
+        uses = jnp.ones((), jnp.float32)
+        for dilation in (DILATION_SECOND, DILATION_THIRD):
+            offset = head_index % dilation
+            row_uses = (row_index % dilation == offset).astype(jnp.float32)
+            key_uses = (key_index % dilation == offset).astype(jnp.float32)
+            uses = uses + row_uses[:, None] * key_uses[None, :]
+        weights = jnp.exp(scores - highest) * uses
+        mass = jnp.sum(weights, axis=1, keepdims=True)
+        summed_values = jnp.dot(
+            weights.astype(jnp.bfloat16), value[:, columns], preferred_element_type=jnp.float32
+        )
+        attended.append(summed_values / mass)
+    combined = jnp.concatenate(attended, axis=1)
+    combined = jnp.where((row_index < valid_limit)[:, None], combined, 0.0)
+    rows_full = lax.all_gather(combined.astype(jnp.bfloat16), "head", axis=1, tiled=True)
+    rows_full = rows_full.astype(jnp.float32)
+    mean_value = jnp.mean(rows_full, axis=1, keepdims=True)
+    mean_square = jnp.mean(rows_full * rows_full, axis=1, keepdims=True)
+    scaling = lax.rsqrt(mean_square - mean_value * mean_value + layer_eps)
+    settled = ((rows_full - mean_value) * scaling * all_gain).astype(jnp.bfloat16)
+    return own_part.astype(jnp.float32) + jnp.dot(
+        settled, out_columns, preferred_element_type=jnp.float32
+    )
+
+
 def solution(mesh):
     placed = (
         P(("groups", "seq"), None, None),
@@ -249,6 +404,12 @@
         P("head"),
         P("head", None),
     )
+
+
+    def route(*arrays):
+        single = arrays[9].shape[0] <= min(SPAN0, SPAN1)
+        return (body_single if single else body)(*arrays)
+
     return jax.shard_map(
-        body, mesh=mesh, in_specs=placed, out_specs=P(("groups", "seq"), "head"), check_vma=False
-    )
+        route, mesh=mesh, in_specs=placed, out_specs=P(("groups", "seq"), "head"), check_vma=False
+    )

time: 282 us -> 209 us (0.74)
  waiting for transfers between devices: 161 us -> 45.1 us
  blocking collectives: 62.7 us -> 97.3 us
  local copies, waits for them, and re-layouts: 12.1 us -> 6.04 us
  matrix products: 11.7 us -> 17.3 us
  starting transfers between devices: 7.51 us -> 13.1 us
  other arithmetic: 11.2 us -> 14.5 us
    all_gather x1, waiting for transfers between devices: 110 us -> 39.3 us  [hidden_means(): gathered = lax.all_gather(w_gate_up, 'seq', axis=1, tiled=True)]
    all_gather x4 -> x6, blocking collectives: 46.9 us -> 90.7 us  [the longest x1 31.6 us: body_single(): key_value_pre = lax.all_gather(projected_pre[1:], 'seq', axis=1, tiled=True)]
    reduce_scatter x1 -> x0, waiting for transfers between devices: 22.4 us -> none  [body(): lax.psum_scatter(partial_rows, 'head', scatter_dimension=1, tiled=True)]
    ppermute x2 -> x0, waiting for transfers between devices: 17.9 us -> none  [from_partner(): return lax.ppermute(value, axis, pairs)]
    psum x2 -> x0, blocking collectives: 15.8 us -> none  [the longest x1 10.1 us: body(): summed = lax.psum(pooled_part, 'head')]
    optimization_barrier x0 -> x1, blocking collectives: none -> 6.62 us  [hidden_means(): gathered, early = lax.optimization_barrier((gathered, early))]
    all_to_all x2 -> x3, starting transfers between devices: 6.58 us -> 13.1 us  [the longest x1 6.35 us: body_single(): lax.all_to_all(outgoing, 'seq', split_axis=0, concat_axis=0, tiled=True)]
    all_to_all x2 -> x3, waiting for transfers between devices: 10.8 us -> 5.09 us  [the longest x1 5.08 us: spread(): lax.all_to_all(jnp.broadcast_to(value[None], (count, *value.shape)), axis...]
  transfers between devices with their start and end apart: 6 -> 4, of which waited for: 6 -> 2; matrix products, arithmetic and copies ran while one was open for 4% -> 7% of each run, Pallas kernels for 0% -> 0%
where the time goes in v1:
time: 209 us
  blocking collectives  97.3 us (47%)
  waiting for transfers between devices  45.1 us (22%)
  matrix products  17.3 us (8%)
  between operations  15.4 us (7%)
  other arithmetic  14.5 us (7%)
  starting transfers between devices  13.1 us (6%)
  local copies, waits for them, and re-layouts  6.04 us (3%)
    all_gather x1, waiting for transfers between devices, hidden_means(): gathered = lax.all_gather(w_gate_up, 'seq', axis=1, tiled=True)  39.3 us
    all_gather x1, blocking collectives, body_single(): key_value_pre = lax.all_gather(projected_pre[1:], 'seq', axis=1, tiled=True)  31.6 us
    all_gather x1, blocking collectives, body_single(): parts = lax.all_gather(local_part, ('seq', 'head'))  19.3 us
    all_gather x1, blocking collectives, body_single(): lax.all_gather(jnp.mean(tile_tokens, axis=1, dtype=jnp.float32), 'seq', a...  17.8 us
    all_gather x1, blocking collectives, body_single(): sequence = lax.all_gather(own_pre, 'head', axis=1, tiled=True)  10 us
    optimization_barrier x1, blocking collectives, hidden_means(): gathered, early = lax.optimization_barrier((gathered, early))  6.62 us
    all_gather x1, blocking collectives, body_single(): lax.all_gather(combined.astype(jnp.bfloat16), 'head', axis=1, tiled=True)  6.56 us
    all_to_all x1, starting transfers between devices, body_single(): lax.all_to_all(outgoing, 'seq', split_axis=0, concat_axis=0, tiled=True)  6.35 us
  transfers between devices with their start and end apart: 4, of which 2 were waited for; matrix products, arithmetic and copies ran while one was open for 7% of the time, Pallas kernels for 0%

profile of v1, /device:TPU:0, one launch (start us, length us, event | category | flops | bytes accessed | tf_op | source)
XLA Modules:
  0.0 208.8 jit_solution(2389834831403494740)
XLA Ops:
  6.5 0.7 all-gather.5.cloned.1.call-update
  7.3 1.0 select_reduce_fusion
  8.6 1.1 convolution_convert_fusion.5
  9.7 0.8 copy.26
  10.4 6.3 %all-to-all-start = ((bf16[4,64,192]{2,1,0:T(8,128)(2,1)}), bf16[4,64,192]{2,1,0:T(8,128)(2,1)S(1)}, u32[]{:S(2)}, u32[]{:S(2)}) async-start(bf16[4,64,192]{2,1,0:T(8,128)(2,1)} %bitcast), calls=%async_computation | async-start | bytes 262144 | tf_op jit(solution)/shard_map/all_to_all | solution.py:293
  17.1 0.7 multiply_reduce_fusion
  18.7 0.6 compare_convert_fusion.6
  19.3 0.6 compare_convert_fusion.4
  19.9 0.6 compare_convert_fusion.2
  20.5 0.6 compare_convert_fusion
  21.1 0.6 fusion.90
  21.7 0.6 fusion.91
  22.6 0.9 iota_compare_fusion
  23.5 1.7 fusion.2
  25.2 17.8 %all-gather.1 = f32[4,2,1536]{2,1,0:T(2,128)S(1)} all-gather(f32[1,2,1536]{2,1,0:T(2,128)S(1)} %multiply_bitcast_fusion), channel_id=1, replica_groups=mesh['groups'=2,'seq'=4,'head'=4] {'seq'}, dimensions={0}, use_global_device_ids=true | all-gather | bytes 61440 | tf_op jit(solution)/shard_map/all_gather | solution.py:312
  43.0 0.6 reshape.291
  43.6 0.9 copy.28
  44.6 0.6 dynamic-slice
  46.0 6.6 %all-reduce.1 = f32[768]{0:T(1024)} all-reduce(f32[768]{0:T(1024)S(1)} %dynamic-update-slice), channel_id=1, replica_groups=mesh['groups'=2,'seq'=4,'head'=4] {'head'}, use_global_device_ids=true, to_apply=%add.1 | all-reduce | flops 768 | bytes 6144 | tf_op jit(solution)/shard_map/optimization_barrier | solution.py:246
  52.6 0.6 fusion.93
  53.2 3.5 %all-to-all-start.1 = ((bf16[192,4,192]{0,2,1:T(8,128)(2,1)}), bf16[192,4,192]{0,2,1:T(8,128)(2,1)S(1)}, u32[]{:S(2)}, u32[]{:S(2)}) async-start(bf16[192,4,192]{0,2,1:T(8,128)(2,1)} %bitcast.6), calls=%async_computation.1 | async-start | bytes 786432 | tf_op jit(solution)/shard_map/all_to_all | solution.py:310
  57.0 10.0 %all_gather.28 = bf16[256,768]{0,1:T(8,128)(2,1)S(1)} all-gather(bf16[256,192]{0,1:T(8,128)(2,1)S(1)} %convolution_convert_fusion.4), channel_id=1, replica_groups=mesh['groups'=2,'seq'=4,'head'=4] {'head'}, dimensions={1}, use_global_device_ids=true | all-gather | bytes 491520 | tf_op jit(solution)/shard_map/all_gather | solution.py:300
  67.3 0.5 fusion.37
  67.9 31.6 %all_gather.29 = bf16[2,1024,192]{1,2,0:T(8,128)(2,1)} all-gather(bf16[2,256,192]{1,2,0:T(8,128)(2,1)S(1)} %slice.84), channel_id=1, replica_groups=mesh['groups'=2,'seq'=4,'head'=4] {'seq'}, dimensions={1}, use_global_device_ids=true | all-gather | bytes 983040 | tf_op jit(solution)/shard_map/all_gather | solution.py:309
  99.8 1.1 all_to_all.31
  100.9 39.3 %all-gather.5.cloned.1.call-done = bf16[2,1536,1024]{2,1,0:T(8,128)(2,1)} async-done(((bf16[2,384,1024]{2,1,0:T(8,128)(2,1)}), bf16[2,1536,1024]{2,1,0:T(8,128)(2,1)}) %all-gather.5.cloned.1.call-update) | async-done | bytes 6291472 | tf_op jit(solution)/shard_map/all_gather | solution.py:245
  140.2 5.5 %convolution_bitcast_fusion = f32[2,512,1024]{2,1,0:T(8,128)S(1)} fusion(bf16[2,1536,1024]{2,1,0:T(8,128)(2,1)} %all-gather.5.cloned.1.call-done, bf16[512,1536]{1,0:T(8,128)(2,1)S(1)} %copy-done.2), kind=kOutput, calls=%fused_computation.7 | convolution fusion | flops 3221225472 | bytes 12058624 | tf_op jit(solution)/shard_map/rk,gkf->grf/dot_general | solution.py:247
  145.7 0.6 fusion.112
  146.4 0.6 convert_reduce_fusion.2
  147.0 0.6 broadcast_in_dim.46
  147.6 3.3 %all-to-all-start.2 = ((f32[4,2,1024]{2,1,0:T(2,128)}), f32[4,2,1024]{2,1,0:T(2,128)S(1)}, u32[]{:S(2)}, u32[]{:S(2)}) async-start(f32[4,2,1024]{2,1,0:T(2,128)} %broadcast_in_dim.46), calls=%async_computation.2 | async-start | bytes 65536 | tf_op jit(solution)/shard_map/all_to_all | solution.py:236
  150.9 0.5 fusion.102
  151.4 5.1 %all-to-all-done.2 = f32[4,2,1024]{2,1,0:T(2,128)S(1)} async-done(((f32[4,2,1024]{2,1,0:T(2,128)}), f32[4,2,1024]{2,1,0:T(2,128)S(1)}, u32[]{:S(2)}, u32[]{:S(2)}) %all-to-all-start.2) | async-done | bytes 32800 | tf_op jit(solution)/shard_map/all_to_all | solution.py:236
  156.9 19.3 %all-gather = f32[128,384]{1,0:T(8,128)S(1)} all-gather(f32[8,384]{1,0:T(8,128)S(1)} %fusion.117), channel_id=2, replica_groups=mesh['groups'=2,'seq'=4,'head'=4] {'seq','head'}, dimensions={0}, use_global_device_ids=true | all-gather | bytes 208896 | tf_op jit(solution)/shard_map/all_gather | solution.py:329
  176.3 0.9 fusion.111
  177.4 1.0 fusion.14
  178.4 5.4 %all-gather.2 = bf16[4,192,8]{1,2,0:T(8,128)(2,1)S(1)} all-gather(bf16[1,192,8]{1,2,0:T(8,128)(2,1)S(1)} %bitcast.90), channel_id=1, replica_groups=mesh['groups'=2,'seq'=4,'head'=4] {'head'}, dimensions={0}, use_global_device_ids=true | all-gather | bytes 15360 | tf_op jit(solution)/shard_map/all_gather | solution.py:337
  184.2 1.1 fusion.13
  185.3 1.2 fusion.8
  186.4 1.1 fusion.9
  189.6 0.5 fusion.24
  190.1 0.5 convolution_divide_fusion.3
  190.7 0.5 fusion.26
  191.7 0.5 fusion.28
  192.2 0.5 convolution_divide_fusion.1
  192.8 0.5 fusion.30
  193.9 6.6 %all_gather.35 = bf16[256,768]{0,1:T(8,128)(2,1)S(1)} all-gather(bf16[256,192]{0,1:T(8,128)(2,1)S(1)} %fusion.48), channel_id=1, replica_groups=mesh['groups'=2,'seq'=4,'head'=4] {'head'}, dimensions={1}, use_global_device_ids=true | all-gather | bytes 491520 | tf_op jit(solution)/shard_map/all_gather | solution.py:378
  200.9 1.0 convolution_add_fusion
  (121 shorter events, 6.6 us)
Async XLA Ops:
  6.5 60.8 %copy-start = (bf16[3,768,192]{1,2,0:T(8,128)(2,1)S(1)}, bf16[3,768,192]{1,2,0:T(8,128)(2,1)}, u32[]{:S(2)}) copy-start(bf16[3,768,192]{1,2,0:T(8,128)(2,1)} %param.27) | copy-start | bytes 2654212
  6.5 10.3 %copy-start.1 = (bf16[2,256,1536]{2,1,0:T(8,128)(2,1)S(1)}, bf16[2,256,1536]{2,1,0:T(8,128)(2,1)}, u32[]{:S(2)}) copy-start(bf16[2,256,1536]{2,1,0:T(8,128)(2,1)} %param.15) | copy-start | bytes 4718596
  6.5 133.7 %all-gather.5.cloned.1.call-start = ((), (), s32[]{:S(2)}) async-start(), calls=%async_computation.3 | async-start | bytes 7864320 | tf_op jit(solution)/shard_map/all_gather | solution.py:245
  7.3 11.3 %copy-start.11 = (s32[1024]{0:T(1024)S(1)}, s32[1024]{0:T(1024)}, u32[]{:S(2)}) copy-start(s32[1024]{0:T(1024)} %param.24) | copy-start | bytes 12292
  8.5 14.9 %copy-start.18 = (f32[1536]{0:T(1024)S(1)}, f32[1536]{0:T(1024)}, u32[]{:S(2)}) copy-start(f32[1536]{0:T(1024)} %param.16) | copy-start | bytes 18436
  10.4 42.8 %all-to-all-start = ((bf16[4,64,192]{2,1,0:T(8,128)(2,1)}), bf16[4,64,192]{2,1,0:T(8,128)(2,1)S(1)}, u32[]{:S(2)}, u32[]{:S(2)}) async-start(bf16[4,64,192]{2,1,0:T(8,128)(2,1)} %bitcast), calls=%async_computation | async-start | bytes 262144 | tf_op jit(solution)/shard_map/all_to_all | solution.py:293
  17.8 25.8 %copy-start.9 = (bf16[192,768]{1,0:T(8,128)(2,1)S(1)}, bf16[192,768]{1,0:T(8,128)(2,1)}, u32[]{:S(2)}) copy-start(bf16[192,768]{1,0:T(8,128)(2,1)} %param.29) | copy-start | bytes 884740
  22.5 22.1 %copy-start.33 = (u32[32]{0:T(128)S(1)}, u32[32]{0:T(128)}, u32[]{:S(2)}) copy-start(u32[32]{0:T(128)} %constant.219) | copy-start | bytes 388
  22.6 2.6 %copy-start.17 = (s32[1024]{0:T(1024)}, s32[1024]{0:T(1024)S(1)}, u32[]{:S(2)}) copy-start(s32[1024]{0:T(1024)S(1)} %fusion.76) | copy-start | bytes 12292
  22.6 23.1 %copy-start.31 = (f32[192]{0:T(256)S(1)}, f32[192]{0:T(256)}, u32[]{:S(2)}) copy-start(f32[192]{0:T(256)} %param.28) | copy-start | bytes 2308
  25.2 42.2 %copy-start.21 = (f32[768]{0:T(1024)S(1)}, f32[768]{0:T(1024)}, u32[]{:S(2)}) copy-start(f32[768]{0:T(1024)} %param.26) | copy-start | bytes 9220
  53.2 46.3 %all-to-all-start.1 = ((bf16[192,4,192]{0,2,1:T(8,128)(2,1)}), bf16[192,4,192]{0,2,1:T(8,128)(2,1)S(1)}, u32[]{:S(2)}, u32[]{:S(2)}) async-start(bf16[192,4,192]{0,2,1:T(8,128)(2,1)} %bitcast.6), calls=%async_computation.1 | async-start | bytes 786432 | tf_op jit(solution)/shard_map/all_to_all | solution.py:310
  57.0 10.3 %copy-start.3 = (bf16[256,192]{0,1:T(8,128)(2,1)}, bf16[256,192]{0,1:T(8,128)(2,1)S(1)}, u32[]{:S(2)}) copy-start(bf16[256,192]{0,1:T(8,128)(2,1)S(1)} %convolution_convert_fusion.4) | copy-start | bytes 294916
  67.9 72.4 %copy-start.2 = (bf16[512,1536]{1,0:T(8,128)(2,1)S(1)}, bf16[512,1536]{1,0:T(8,128)(2,1)}, u32[]{:S(2)}) copy-start(bf16[512,1536]{1,0:T(8,128)(2,1)} %fusion.2) | copy-start | bytes 4718596
  146.3 10.2 %copy-start.5 = (bf16[1024,384]{1,0:T(8,128)(2,1)S(1)}, bf16[1024,384]{1,0:T(8,128)(2,1)}, u32[]{:S(2)}) copy-start(bf16[1024,384]{1,0:T(8,128)(2,1)} %param.18) | copy-start | bytes 2359300
  146.3 29.9 %copy-start.20 = (f32[1536]{0:T(1024)S(1)}, f32[1536]{0:T(1024)}, u32[]{:S(2)}) copy-start(f32[1536]{0:T(1024)} %param.19) | copy-start | bytes 18436
  146.4 31.1 %copy-start.7 = (bf16[1536,192]{0,1:T(8,128)(2,1)S(1)}, bf16[1536,192]{0,1:T(8,128)(2,1)}, u32[]{:S(2)}) copy-start(bf16[1536,192]{0,1:T(8,128)(2,1)} %param.21) | copy-start | bytes 1769476
  146.4 31.1 %copy-start.19 = (f32[1536]{0:T(1024)S(1)}, f32[1536]{0:T(1024)}, u32[]{:S(2)}) copy-start(f32[1536]{0:T(1024)} %param.20) | copy-start | bytes 18436
  147.0 38.3 %copy-start.6 = (bf16[2,1024,192]{1,2,0:T(8,128)(2,1)S(1)}, bf16[2,1024,192]{1,2,0:T(8,128)(2,1)}, u32[]{:S(2)}) copy-start(bf16[2,1024,192]{1,2,0:T(8,128)(2,1)} %all_gather.29) | copy-start | bytes 2359300
  147.6 8.9 %all-to-all-start.2 = ((f32[4,2,1024]{2,1,0:T(2,128)}), f32[4,2,1024]{2,1,0:T(2,128)S(1)}, u32[]{:S(2)}, u32[]{:S(2)}) async-start(f32[4,2,1024]{2,1,0:T(2,128)} %broadcast_in_dim.46), calls=%async_computation.2 | async-start | bytes 65536 | tf_op jit(solution)/shard_map/all_to_all | solution.py:236
  156.9 30.7 %copy-start.8 = (pred[1024,8]{1,0:T(32,128)(4,1)S(1)}, pred[1024,8]{1,0:T(32,128)(4,1)}, u32[]{:S(2)}) copy-start(pred[1024,8]{1,0:T(32,128)(4,1)} %iota_compare_fusion) | copy-start | bytes 24580
  187.9 1.7 copy-start.13
  187.9 1.7 copy-start.14
  187.9 1.7 copy-start.29
  187.9 1.7 copy-start.30
  189.1 1.5 copy-start.12
  189.1 1.5 copy-start.27
  189.1 1.5 copy-start.28
  190.6 1.1 copy-start.25
  190.6 1.1 copy-start.26
  191.7 1.1 copy-start.15
  191.7 1.1 copy-start.16
  191.7 1.1 copy-start.23
  191.7 1.1 copy-start.24
  192.8 1.1 copy-start.32
  192.8 7.8 %copy-start.4 = (bf16[256,192]{0,1:T(8,128)(2,1)S(1)}, bf16[256,192]{0,1:T(8,128)(2,1)}, u32[]{:S(2)}) copy-start(bf16[256,192]{0,1:T(8,128)(2,1)} %copy-done.3) | copy-start | bytes 294916
  193.3 7.5 %copy-start.10 = (bf16[768,192]{0,1:T(8,128)(2,1)S(1)}, bf16[768,192]{0,1:T(8,128)(2,1)}, u32[]{:S(2)}) copy-start(bf16[768,192]{0,1:T(8,128)(2,1)} %all_to_all.31) | copy-start | bytes 884740
  193.3 7.5 %copy-start.22 = (f32[768]{0:T(1024)S(1)}, f32[768]{0:T(1024)}, u32[]{:S(2)}) copy-start(f32[768]{0:T(1024)} %all-reduce.1) | copy-start | bytes 9220
Sparse Core Ops, SparseCore 0:
  8.9 131.2 all-gather.4
